TPU v7x, 32 devices: a whole 2x2x4 slice. The times are simulated.
32 devices in a mesh: dp: 4 (over x, core), space: 8 (over z, y).
Axes of the slice: x: 2, y: 2, z: 4, core: 2. Of those that a mesh axis runs over, the one named last changes fastest.
Arguments:
- section_three: bfloat16 [4, 64, 128, 512], P('dp', 'space'), parts along dimension 0, may hold values from -6 to 6
- section_four: bfloat16 [4, 32, 64, 1024], P('dp', 'space'), parts along dimension 0, may hold values from -6 to 6
- section_five: bfloat16 [4, 16, 32, 2048], P('dp', 'space'), parts along dimension 0, may hold values from -6 to 6
- lateral_three: bfloat16 [512, 256], P('space'), may hold values from -0.25 to 0.25
- lateral_four: bfloat16 [1024, 256], P('space'), may hold values from -0.1875 to 0.1875
- lateral_five: bfloat16 [2048, 256], P('space'), may hold values from -0.125 to 0.125
- lateral_bias_three: float32 [256], replicated, may hold values from -3 to 3
- lateral_bias_four: float32 [256], replicated, may hold values from -3 to 3
- lateral_bias_five: float32 [256], replicated, may hold values from -3 to 3
- output_three: bfloat16 [3, 3, 256, 256], P(None, None, 'space'), may hold values from -0.125 to 0.125
- output_four: bfloat16 [3, 3, 256, 256], P(None, None, 'space'), may hold values from -0.125 to 0.125
- output_five: bfloat16 [3, 3, 256, 256], P(None, None, 'space'), may hold values from -0.125 to 0.125
- output_bias_three: float32 [256], replicated, may hold values from -3 to 3
- output_bias_four: float32 [256], replicated, may hold values from -3 to 3
- output_bias_five: float32 [256], replicated, may hold values from -3 to 3
Outputs:
- level_three: bfloat16 [4, 64, 128, 256], P('dp', 'space'), parts along dimension 0
- level_four: bfloat16 [4, 32, 64, 256], P('dp', 'space'), parts along dimension 0
- level_five: bfloat16 [4, 16, 32, 256], P('dp'), parts along dimension 0
- level_six: bfloat16 [4, 8, 16, 256], P('dp'), parts along dimension 0
There are 4 independent parts, one for each index of `dp`. A program takes and returns all parts, laid end to end along the dimension named above; an argument that names none is the same for every part. Nothing has to cross between parts.
All inputs are finite; a program needn't handle non-finite values.
Results may differ from a plain program's by a relative error of at most 0.0095.
Values may be sent and summed in bfloat16 or wider, within the bound.
A program may use at most 64 MiB of HBM per device.

v0:
```python
import jax
import jax.numpy as jnp
from jax import lax
from jax.sharding import PartitionSpec as P


def with_halo(cells, sides, width):
    for axis, dim in sides:
        count = lax.axis_size(axis)
        ends = count - 1
        head = lax.slice_in_dim(cells, 0, width, axis=dim)
        tail = lax.slice_in_dim(cells, cells.shape[dim] - width, cells.shape[dim], axis=dim)
        cells = jnp.concatenate(
            [
                lax.ppermute(tail, axis, [(i, (i + 1) % count) for i in range(ends)]),
                cells,
                lax.ppermute(head, axis, [((i + 1) % count, i) for i in range(ends)]),
            ],
            axis=dim,
        )
    return cells


def lateral(features, weight, offset):
    images, rows, columns, channels = features.shape
    summed = (
        jnp.dot(features.reshape(-1, channels), weight, preferred_element_type=jnp.float32) + offset
    )
    return summed.reshape(images, rows, columns, -1)


def enlarge(coarse):
    return jnp.repeat(jnp.repeat(coarse, 2, axis=1), 2, axis=2)


def conv_rows(padded, weight, offset):
    images, rows_in, columns, channels = padded.shape
    height = rows_in - 2
    framed = jnp.pad(padded, ((0, 0), (0, 0), (1, 1), (0, 0)))
    summed = jnp.zeros((images * height * columns, weight.shape[3]), jnp.float32)
    for row_off in range(3):
        for col_off in range(3):
            window = framed[:, row_off : row_off + height, col_off : col_off + columns, :].reshape(
                -1, channels
            )
            summed = summed + jnp.dot(
                window, weight[row_off, col_off], preferred_element_type=jnp.float32
            )
    return (summed + offset).reshape(images, height, columns, -1).astype(jnp.bfloat16)


def on_device(
    section_three,
    section_four,
    section_five,
    lateral_three,
    lateral_four,
    lateral_five,
    lateral_bias_three,
    lateral_bias_four,
    lateral_bias_five,
    output_three,
    output_four,
    output_five,
    output_bias_three,
    output_bias_four,
    output_bias_five,
):
    whole_lat3, whole_lat4, whole_lat5, whole_out3, whole_out4, whole_out5 = (
        lax.all_gather(lateral_three, "space", axis=0, tiled=True),
        lax.all_gather(lateral_four, "space", axis=0, tiled=True),
        lax.all_gather(lateral_five, "space", axis=0, tiled=True),
        lax.all_gather(output_three, "space", axis=2, tiled=True),
        lax.all_gather(output_four, "space", axis=2, tiled=True),
        lax.all_gather(output_five, "space", axis=2, tiled=True),
    )
    merged_five = lateral(section_five, whole_lat5, lateral_bias_five).astype(jnp.bfloat16)
    merged_four = (
        lateral(section_four, whole_lat4, lateral_bias_four)
        + enlarge(merged_five).astype(jnp.float32)
    ).astype(jnp.bfloat16)
    merged_three = (
        lateral(section_three, whole_lat3, lateral_bias_three)
        + enlarge(merged_four).astype(jnp.float32)
    ).astype(jnp.bfloat16)
    rimmed_three = with_halo(merged_three, (("space", 1),), 1)
    rimmed_four = with_halo(merged_four, (("space", 1),), 1)
    level_three = conv_rows(rimmed_three, whole_out3, output_bias_three)
    level_four = conv_rows(rimmed_four, whole_out4, output_bias_four)
    whole_five = lax.all_gather(merged_five, "space", axis=1, tiled=True)
    padded_five = jnp.pad(whole_five, ((0, 0), (1, 1), (0, 0), (0, 0)))
    level_five = conv_rows(padded_five, whole_out5, output_bias_five)
    level_six = level_five[:, ::2, ::2, :]
    return (level_three, level_four, level_five, level_six)


def solution(mesh):
    return jax.shard_map(
        on_device,
        mesh=mesh,
        in_specs=(
            P("dp", "space", None, None),
            P("dp", "space", None, None),
            P("dp", "space", None, None),
            P("space", None),
            P("space", None),
            P("space", None),
            P(),
            P(),
            P(),
            P(None, None, "space", None),
            P(None, None, "space", None),
            P(None, None, "space", None),
            P(),
            P(),
            P(),
        ),
        out_specs=(
            P("dp", "space", None, None),
            P("dp", "space", None, None),
            P("dp", None, None, None),
            P("dp", None, None, None),
        ),
        check_vma=False,
    )
```

profile of v0, /device:TPU:0, one launch (start us, length us, event | category | flops | bytes accessed | tf_op | source)
XLA Modules:
  0.0 203.1 jit_solution(6566703507592191311)
XLA Ops:
  10.0 33.9 %all_gather.22 = bf16[1024,256]{1,0:T(8,128)(2,1)S(1)} all-gather(bf16[128,256]{1,0:T(8,128)(2,1)} %param.19), channel_id=1, replica_groups=mesh['dp'=4,'space'=8] {'space'}, dimensions={0}, use_global_device_ids=true | all-gather | bytes 589824 | tf_op jit(solution)/shard_map/all_gather | solution.py:71
  43.9 30.8 %all_gather.21 = bf16[512,256]{1,0:T(8,128)(2,1)S(1)} all-gather(bf16[64,256]{1,0:T(8,128)(2,1)S(1)} %copy-done.36), channel_id=1, replica_groups=mesh['dp'=4,'space'=8] {'space'}, dimensions={0}, use_global_device_ids=true | all-gather | bytes 294912 | tf_op jit(solution)/shard_map/all_gather | solution.py:70
  76.0 1.5 fusion.9
  79.4 4.7 %collective-permute-start.2 = (bf16[1,1,64,256]{3,2,1,0:T(8,128)(2,1)}, bf16[1,1,64,256]{3,2,1,0:T(8,128)(2,1)}, u32[]{:S(2)}, u32[]{:S(2)}) collective-permute-start(bf16[1,1,64,256]{3,2,1,0:T(8,128)(2,1)} %get-tuple-element.30), channel_id=1, source_target_pairs={{0,1},{1,2},{2,3},{3,4},{4,5},{5,6},{6,7},{8,9},{9,10},{10,11},{11... | collective-permute-start | bytes 98312 | tf_op jit(solution)/shard_map/ppermute | solution.py:15
  84.1 1.3 collective-permute-start.3
  85.8 1.7 convert_element_type.169
  87.6 1.3 add_convert_fusion.1
  88.9 0.8 copy-done.1
  90.4 5.2 %collective-permute-start = (bf16[1,1,128,256]{3,2,1,0:T(8,128)(2,1)}, bf16[1,1,128,256]{3,2,1,0:T(8,128)(2,1)}, u32[]{:S(2)}, u32[]{:S(2)}) collective-permute-start(bf16[1,1,128,256]{3,2,1,0:T(8,128)(2,1)} %get-tuple-element.12), channel_id=1, source_target_pairs={{0,1},{1,2},{2,3},{3,4},{4,5},{5,6},{6,7},{8,9},{9,10},{10,11},{11... | collective-permute-start | bytes 196616 | tf_op jit(solution)/shard_map/ppermute | solution.py:15
  95.6 1.3 collective-permute-start.1
  96.8 31.6 %all_gather.26 = bf16[1,16,32,256]{3,2,0,1:T(8,128)(2,1)S(1)} all-gather(bf16[1,2,32,256]{3,2,0,1:T(8,128)(2,1)S(1)} %bitcast.189), channel_id=1, replica_groups=mesh['dp'=4,'space'=8] {'space'}, dimensions={1}, use_global_device_ids=true | all-gather | bytes 294912 | tf_op jit(solution)/shard_map/all_gather | solution.py:90
  128.5 1.3 pad_slice_fusion
  129.8 0.9 pad_slice_fusion.6
  130.7 1.9 convert_element_type.177
  132.6 1.7 convert_element_type.171
  134.3 0.9 fusion.20
  135.2 0.9 fusion.29
  136.1 1.5 pad_maximum_fusion.2
  137.6 1.1 fusion.14
  138.7 1.6 fusion.27
  140.3 1.9 pad_maximum_fusion
  142.2 1.3 fusion.22
  143.6 1.2 convolution_add_fusion.15
  147.5 2.5 %slice.239 = bf16[1,8,16,256]{3,2,1,0:T(8,128)(2,1)} slice(bf16[1,16,32,256]{3,2,1,0:T(8,128)(2,1)S(1)} %bitcast.186), slice={[0:1:1], [0:16:2], [0:32:2], [0:256:1]} | slice | bytes 131072 | tf_op jit(solution)/shard_map/slice | solution.py:93
  150.1 1.1 fusion.24
  151.2 1.8 fusion.23
  153.1 30.5 %all-gather.7.cloned.1.call-done = bf16[3,3,256,256]{3,2,1,0:T(8,128)(2,1)} async-done(((bf16[3,3,32,256]{3,2,1,0:T(8,128)(2,1)}), bf16[3,3,256,256]{3,2,1,0:T(8,128)(2,1)}) %all-gather.7.cloned.1.call-update) | async-done | bytes 1179664 | tf_op jit(solution)/shard_map/all_gather | solution.py:73
  183.5 1.3 fusion.26
  185.2 0.9 copy-done.13
  190.6 0.9 copy-done.6
  194.6 0.9 fusion.8
  195.5 1.1 fusion.3
  (131 shorter events, 17.4 us)
Async XLA Ops:
  7.2 67.8 %copy-start = (bf16[1,8,128,512]{3,2,1,0:T(8,128)(2,1)S(1)}, bf16[1,8,128,512]{3,2,1,0:T(8,128)(2,1)}, u32[]{:S(2)}) copy-start(bf16[1,8,128,512]{3,2,1,0:T(8,128)(2,1)} %param.15) | copy-start | bytes 3145732
  7.2 36.7 %copy-start.36 = (bf16[64,256]{1,0:T(8,128)(2,1)S(1)}, bf16[64,256]{1,0:T(8,128)(2,1)}, u32[]{:S(2)}) copy-start(bf16[64,256]{1,0:T(8,128)(2,1)} %param.18) | copy-start | bytes 98308
  7.2 67.5 %copy-start.24 = (bf16[1,4,64,1024]{3,2,1,0:T(8,128)(2,1)S(1)}, bf16[1,4,64,1024]{3,2,1,0:T(8,128)(2,1)}, u32[]{:S(2)}) copy-start(bf16[1,4,64,1024]{3,2,1,0:T(8,128)(2,1)} %param.16) | copy-start | bytes 1572868
  7.2 67.5 %copy-start.40 = (f32[256]{0:T(256)S(1)}, f32[256]{0:T(256)}, u32[]{:S(2)}) copy-start(f32[256]{0:T(256)} %param.22) | copy-start | bytes 3076
  7.2 68.3 %all-gather.5.cloned.1.call-start = ((), (), s32[]{:S(2)}) async-start(), calls=%async_computation | async-start | bytes 1179648 | tf_op jit(solution)/shard_map/all_gather | solution.py:72
  7.9 134.3 %all-gather.11.cloned.1.call-start = ((), (), s32[]{:S(2)}) async-start(), calls=%async_computation.3 | async-start | bytes 1327104 | tf_op jit(solution)/shard_map/all_gather | solution.py:75
  8.7 141.4 %all-gather.9.cloned.1.call-start = ((), (), s32[]{:S(2)}) async-start(), calls=%async_computation.2 | async-start | bytes 1327104 | tf_op jit(solution)/shard_map/all_gather | solution.py:74
  9.4 65.6 %copy-start.37 = (f32[256]{0:T(256)S(1)}, f32[256]{0:T(256)}, u32[]{:S(2)}) copy-start(f32[256]{0:T(256)} %param.21) | copy-start | bytes 3076
  9.4 174.1 %all-gather.7.cloned.1.call-start = ((), (), s32[]{:S(2)}) async-start(), calls=%async_computation.1 | async-start | bytes 1327104 | tf_op jit(solution)/shard_map/all_gather | solution.py:73
  75.0 10.4 %copy-start.4 = (f32[256,256]{1,0:T(8,128)}, f32[256,256]{1,0:T(8,128)S(1)}, u32[]{:S(2)}) copy-start(f32[256,256]{1,0:T(8,128)S(1)} %convolution_add_fusion.23) | copy-start | bytes 786436
  75.0 1.0 copy-start.35
  78.3 7.1 %copy-start.3 = (f32[4,32,2,256]{3,2,1,0:T(2,128)}, f32[4,32,2,256]{3,2,1,0:T(2,128)S(1)}, u32[]{:S(2)}) copy-start(f32[4,32,2,256]{3,2,1,0:T(2,128)S(1)} %broadcast_in_dim.9) | copy-start | bytes 786436
  79.4 55.0 %collective-permute-start.2 = (bf16[1,1,64,256]{3,2,1,0:T(8,128)(2,1)}, bf16[1,1,64,256]{3,2,1,0:T(8,128)(2,1)}, u32[]{:S(2)}, u32[]{:S(2)}) collective-permute-start(bf16[1,1,64,256]{3,2,1,0:T(8,128)(2,1)} %get-tuple-element.30), channel_id=1, source_target_pairs={{0,1},{1,2},{2,3},{3,4},{4,5},{5,6},{6,7},{8,9},{9,10},{10,11},{11... | collective-permute-start | bytes 98312 | tf_op jit(solution)/shard_map/ppermute | solution.py:15
  84.1 50.2 %collective-permute-start.3 = (bf16[1,1,64,256]{3,2,1,0:T(8,128)(2,1)}, bf16[1,1,64,256]{3,2,1,0:T(8,128)(2,1)}, u32[]{:S(2)}, u32[]{:S(2)}) collective-permute-start(bf16[1,1,64,256]{3,2,1,0:T(8,128)(2,1)} %get-tuple-element.31), channel_id=1, source_target_pairs={{1,0},{2,1},{3,2},{4,3},{5,4},{6,5},{7,6},{9,8},{10,9},{11,10},{12... | collective-permute-start | bytes 98312 | tf_op jit(solution)/shard_map/ppermute | solution.py:17
  87.6 9.3 %copy-start.34 = (bf16[64,256]{1,0:T(8,128)(2,1)S(1)}, bf16[64,256]{1,0:T(8,128)(2,1)}, u32[]{:S(2)}) copy-start(bf16[64,256]{1,0:T(8,128)(2,1)} %copy-done.33) | copy-start | bytes 98308
  90.4 47.2 %collective-permute-start = (bf16[1,1,128,256]{3,2,1,0:T(8,128)(2,1)}, bf16[1,1,128,256]{3,2,1,0:T(8,128)(2,1)}, u32[]{:S(2)}, u32[]{:S(2)}) collective-permute-start(bf16[1,1,128,256]{3,2,1,0:T(8,128)(2,1)} %get-tuple-element.12), channel_id=1, source_target_pairs={{0,1},{1,2},{2,3},{3,4},{4,5},{5,6},{6,7},{8,9},{9,10},{10,11},{11... | collective-permute-start | bytes 196616 | tf_op jit(solution)/shard_map/ppermute | solution.py:15
  95.6 42.1 %collective-permute-start.1 = (bf16[1,1,128,256]{3,2,1,0:T(8,128)(2,1)}, bf16[1,1,128,256]{3,2,1,0:T(8,128)(2,1)}, u32[]{:S(2)}, u32[]{:S(2)}) collective-permute-start(bf16[1,1,128,256]{3,2,1,0:T(8,128)(2,1)} %get-tuple-element.13), channel_id=1, source_target_pairs={{1,0},{2,1},{3,2},{4,3},{5,4},{6,5},{7,6},{9,8},{10,9},{11,10},{12... | collective-permute-start | bytes 196616 | tf_op jit(solution)/shard_map/ppermute | solution.py:17
  134.3 3.3 %copy-start.2 = (bf16[1,8,128,256]{3,2,1,0:T(8,128)(2,1)S(1)}, bf16[1,8,128,256]{3,2,1,0:T(8,128)(2,1)}, u32[]{:S(2)}) copy-start(bf16[1,8,128,256]{3,2,1,0:T(8,128)(2,1)} %copy-done.1) | copy-start | bytes 1572868
  142.2 2.6 %copy-start.14 = (bf16[3,3,256,256]{3,2,1,0:T(8,128)(2,1)S(1)}, bf16[3,3,256,256]{3,2,1,0:T(8,128)(2,1)}, u32[]{:S(2)}) copy-start(bf16[3,3,256,256]{3,2,1,0:T(8,128)(2,1)} %all-gather.11.cloned.1.call-done) | copy-start | bytes 3538948
  142.2 2.6 %copy-start.21 = (bf16[1,16,32,256]{3,2,0,1:T(8,128)(2,1)S(1)}, bf16[1,16,32,256]{3,2,0,1:T(8,128)(2,1)}, u32[]{:S(2)}) copy-start(bf16[1,16,32,256]{3,2,0,1:T(8,128)(2,1)} %get-tuple-element.17) | copy-start | bytes 786436
  143.6 1.5 copy-start.20
  147.2 4.0 %copy-start.31 = (bf16[1,4,64,256]{3,2,1,0:T(8,128)(2,1)S(1)}, bf16[1,4,64,256]{3,2,1,0:T(8,128)(2,1)}, u32[]{:S(2)}) copy-start(bf16[1,4,64,256]{3,2,1,0:T(8,128)(2,1)} %get-tuple-element.27) | copy-start | bytes 393220
  147.5 2.6 %copy-start.32 = (bf16[512,256]{1,0:T(8,128)(2,1)}, bf16[512,256]{1,0:T(8,128)(2,1)S(1)}, u32[]{:S(2)}) copy-start(bf16[512,256]{1,0:T(8,128)(2,1)S(1)} %fusion.5) | copy-start | bytes 786436
  183.5 1.3 copy-start.15
  184.8 1.3 copy-start.13
  184.8 1.3 copy-start.30
  184.8 1.4 copy-start.29
  185.1 1.4 copy-start.28
  187.1 1.1 copy-start.12
  190.3 1.2 copy-start.6
  193.6 1.8 copy-start.11
  193.7 1.8 copy-start.39
  (19 other events, 18.2 us)
Sparse Core Ops, SparseCore 0:
  10.1 44.0 all-gather.4
  56.4 42.5 all-gather.10
  101.2 40.1 all-gather.8
  143.5 39.9 all-gather.6
where the time goes:
time: 204 us; the launch traced here: 203 us
  blocking collectives  96.2 us (47%)
  waiting for transfers between devices  33.1 us (16%)
  local copies, waits for them, and re-layouts  24.3 us (12%)
  matrix products  15.8 us (8%)
  between operations  14.3 us (7%)
  starting transfers between devices  12.6 us (6%)
  other arithmetic  6.78 us (3%)
    all_gather x1, blocking collectives, on_device(): lax.all_gather(lateral_four, 'space', axis=0, tiled=True)  33.9 us
    all_gather x1, blocking collectives, on_device(): whole_five = lax.all_gather(merged_five, 'space', axis=1, tiled=True)  31.6 us
    all_gather x1, blocking collectives, on_device(): lax.all_gather(lateral_three, 'space', axis=0, tiled=True)  30.8 us
    all_gather x1, waiting for transfers between devices, on_device(): lax.all_gather(output_three, 'space', axis=2, tiled=True)  30.5 us
    dot_general x27, matrix products, conv_rows(): jnp.dot(window, weight[row_off, col_off], preferred_element_type=jnp.floa...  13.5 us
    ppermute x2, starting transfers between devices, with_halo(): lax.ppermute(tail, axis, [(i, (i + 1) % count) for i in range(ends)])  9.9 us
    unnamed x86, local copies, waits for them, and re-layouts  9.46 us
    concatenate x4, other arithmetic, with_halo(): jnp.concatenate([lax.ppermute(tail, axis, [(i, (i + 1) % count) for i in...  5.37 us
  transfers between devices with their start and end apart: 8, of which 1 were waited for; matrix products, arithmetic and copies ran while one was open for 15% of the time, Pallas kernels for 0%

commit v1 on v0

v1 whole, which is shorter than its diff:
```python
import functools

import jax
import jax.numpy as jnp
from jax import lax
from jax.experimental import pallas as pl
from jax.experimental.pallas import tpu as pltpu
from jax.sharding import PartitionSpec as P

F32, BF16 = jnp.float32, jnp.bfloat16


def ring_place(s, n):
    return s // 2 + (s % 2) * (n - 1 - 2 * (s // 2))


def ring_owner(place, n):
    r = (place + 2 * n) % n
    back = r // (n // 2)
    return (1 - back) * (2 * r) + back * (2 * (n - 1 - r) + 1)


def spread(coarse):
    pixels = coarse.shape[0]
    fine = lax.broadcasted_iota(jnp.int32, (2 * pixels, pixels), 0) // 2
    pick = (fine == lax.broadcasted_iota(jnp.int32, (2 * pixels, pixels), 1)).astype(BF16)
    return jnp.dot(pick, coarse, preferred_element_type=F32)


def conv_tile(frame, weight, bias, start, pixels, width):
    rows = jnp.concatenate(
        [frame[pl.ds(pl.multiple_of(start + a * width, 16), pixels), :] for a in range(3)], axis=1
    )
    depth = weight.shape[2]
    part = [
        jnp.dot(
            rows,
            weight[:, c].reshape(3 * depth, weight.shape[3]),
            preferred_element_type=F32,
        )
        for c in range(3)
    ]
    column = lax.broadcasted_iota(jnp.int32, (pixels, 1), 0) % width
    left = jnp.where(column == 0, 0.0, pltpu.roll(part[0], 1, 0))
    right = jnp.where(column == width - 1, 0.0, pltpu.roll(part[2], pixels - 1, 0))
    return part[1] + left + right + bias[...]


def kernel(
    n, dims,
    s3, s4, s5, l3, l4, l5, lb3, lb4, lb5, o3, o4, o5, ob3, ob4, ob5,
    y3, y4, y5, y6,
    v3, v4, v5, w_l5, w_l4, w_l3, w_o3, w_o5, w_o4,
    m3, m4, m5, r3, r4, r5, r6,
    ring_send, ring_recv, core_send, core_recv, halo_send, halo_recv, local_sem,
):
    (rows3, wid3), (rows4, wid4), (rows5, wid5) = dims
    dp, s = lax.axis_index("dp"), lax.axis_index("space")
    core = dp % 2
    partner = (dp + 1 - 2 * core, s)
    place = ring_place(s, n)
    sign = 1 - 2 * core
    hops = (n // 2, n - 1 - n // 2)
    turn = (sign, -sign)
    target = [(dp, ring_owner(place + turn[k], n)) for k in range(2)]
    above, below = (dp, (s + n - 1) % n), (dp, (s + 1) % n)

    full = (w_l5, w_l4, w_l3, w_o3, w_o5, w_o4, m5)
    mine = (l5, l4, l3, o3, o5, o4)
    half = w_l5.shape[1] // 2
    MAP = 6

    def chunk(a, owner, side):
        cols = pl.ds(pl.multiple_of(side * half, half), half)
        if a == MAP:
            size = rows5 * wid5
            return m5.at[pl.ds(pl.multiple_of(wid5 + owner * size, 16), size), :]
        if a < 3:
            size = mine[a].shape[0]
            return full[a].at[pl.ds(pl.multiple_of(owner * size, size), size), cols]
        size = mine[a].shape[2]
        return full[a].at[:, :, pl.ds(pl.multiple_of(owner * size, size), size), cols]

    def own_part(a):
        cols = pl.ds(pl.multiple_of(core * half, half), half)
        return mine[a].at[:, cols] if a < 3 else mine[a].at[:, :, :, cols]

    def own_whole(a):
        if a < 3:
            size = mine[a].shape[0]
            return full[a].at[pl.ds(pl.multiple_of(s * size, size), size), :]
        size = mine[a].shape[2]
        return full[a].at[:, :, pl.ds(pl.multiple_of(s * size, size), size), :]

    local = [pltpu.make_async_copy(mine[a], own_whole(a), local_sem.at[a]) for a in range(6)]
    features = [
        pltpu.make_async_copy(src, dst, local_sem.at[6 + k])
        for k, (src, dst) in enumerate(((s5, v5), (s4, v4), (s3, v3)))
    ]
    for copy in features + local:
        copy.start()

    barrier = pltpu.get_barrier_semaphore()
    for device in (target[0], target[1], partner, above, below):
        pl.semaphore_signal(
            barrier, inc=1, device_id=device, device_id_type=pl.DeviceIdType.MESH
        )
    pl.semaphore_wait(barrier, 5)

    def remote(src, dst, send, recv, device):
        return pltpu.make_async_remote_copy(
            src_ref=src, dst_ref=dst, send_sem=send, recv_sem=recv,
            device_id=device, device_id_type=pl.DeviceIdType.MESH,
        )

    sent = []

    def push(a, k, step):
        if step > hops[k]:
            return
        owner = ring_owner(place - turn[k] * (step - 1), n)
        dst = chunk(a, owner, core)
        src = own_part(a) if step == 1 and a != MAP else dst
        copy = remote(src, dst, ring_send.at[a, k, step - 1], ring_recv.at[a, k, step - 1], target[k])
        copy.start()
        sent.append(copy)

    def cross(a, k, step, side, turns):
        owner = ring_owner(place - turns[k] * step, n)
        spot = chunk(a, owner, side)
        j = k * hops[0] + step - 1
        return remote(spot, spot, core_send.at[a, j], core_recv.at[a, j], partner)

    def pull(a, step):
        for k in range(2):
            if step > hops[k]:
                continue
            owner = ring_owner(place - turn[k] * step, n)
            spot = chunk(a, owner, core)
            remote(
                spot, spot, ring_send.at[a, k, step - 1], ring_recv.at[a, k, step - 1], target[k]
            ).wait_recv()
            push(a, k, step + 1)
            if a != MAP:
                copy = cross(a, k, step, core, turn)
                copy.start()
                sent.append(copy)

    def settle(a):
        for k in range(2):
            for step in range(1, hops[k] + 1):
                cross(a, k, step, 1 - core, (turn[1], turn[0])).wait_recv()
        local[a].wait()

    for a in (0, 1, 2):
        push(a, 0, 1)
        push(a, 1, 1)
    waiting = [3, 4, 5]
    for step in range(1, hops[0] + 1):
        if waiting:
            a = waiting.pop(0)
            push(a, 0, 1)
            push(a, 1, 1)
        for a in (0, 1, 2):
            pull(a, step)
    while waiting:
        a = waiting.pop(0)
        push(a, 0, 1)
        push(a, 1, 1)
    for a in (3, 4, 5):
        pull(a, 1)

    settle(0)
    features[0].wait()
    zero5 = jnp.zeros((wid5, m5.shape[1]), BF16)
    m5[pl.ds(0, wid5), :] = zero5
    m5[pl.ds(m5.shape[0] - wid5, wid5), :] = zero5
    here = pl.multiple_of(wid5 + s * (rows5 * wid5), 16)
    m5[pl.ds(here, rows5 * wid5), :] = (
        jnp.dot(v5[...], w_l5[...], preferred_element_type=F32) + lb5[...]
    ).astype(BF16)
    settle(1)
    features[1].wait()
    for r in range(rows5):
        up = spread(m5[pl.ds(pl.multiple_of(here + r * wid5, 16), wid5), :])
        base = 2 * r * wid4
        lat = jnp.dot(v4[base : base + 2 * wid4, :], w_l4[...], preferred_element_type=F32)
        m4[wid4 + base : wid4 + base + 2 * wid4, :] = (
            lat + lb4[...] + jnp.concatenate([up, up], axis=0)
        ).astype(BF16)
    push(MAP, 0, 1)
    push(MAP, 1, 1)
    settle(2)
    features[2].wait()

    def coarse_row(r, carry):
        up = spread(m4[pl.ds(pl.multiple_of(wid4 + r * wid4, 16), wid4), :])
        base = pl.multiple_of(2 * r * wid3, 16)
        lat = jnp.dot(v3[pl.ds(base, 2 * wid3), :], w_l3[...], preferred_element_type=F32)
        m3[pl.ds(pl.multiple_of(wid3 + base, 16), 2 * wid3), :] = (
            lat + lb3[...] + jnp.concatenate([up, up], axis=0)
        ).astype(BF16)
        return carry

    lax.fori_loop(0, rows4, coarse_row, 0)

    halos = []
    for k, (frame, rows, wid) in enumerate(((m4, rows4, wid4), (m3, rows3, wid3))):
        first, last = frame.at[pl.ds(wid, wid), :], frame.at[pl.ds(rows * wid, wid), :]
        top, bottom = frame.at[pl.ds(0, wid), :], frame.at[pl.ds((rows + 1) * wid, wid), :]
        halos.append((
            remote(last, top, halo_send.at[2 * k], halo_recv.at[2 * k], below),
            remote(first, bottom, halo_send.at[2 * k + 1], halo_recv.at[2 * k + 1], above),
        ))
    for step in range(2, hops[0]):
        for a in (3, 4, 5):
            pull(a, step)
        if step == 2:
            for pair in halos:
                for copy in pair:
                    copy.start()
        pull(MAP, step - 1)
    pull(3, hops[0])

    for pair, frame, rows, wid in zip(halos, (m4, m3), (rows4, rows3), (wid4, wid3)):
        for copy in pair:
            copy.wait_recv()
            sent.append(copy)
        zero = jnp.zeros((wid, frame.shape[1]), BF16)

        @pl.when(s == 0)
        def _():
            frame[pl.ds(0, wid), :] = zero

        @pl.when(s == n - 1)
        def _():
            frame[pl.ds((rows + 1) * wid, wid), :] = zero

    settle(3)

    def conv(frame, weight, bias, out, rows, wid, tall):
        def tile(i, carry):
            start = pl.multiple_of(i * (tall * wid), 16)
            out[pl.ds(start, tall * wid), :] = conv_tile(
                frame, weight, bias, start, tall * wid, wid
            ).astype(BF16)
            return carry

        lax.fori_loop(0, rows // tall, tile, 0)

    conv(m3, w_o3, ob3, r3, rows3, wid3, 2)
    out3 = pltpu.make_async_copy(r3, y3, local_sem.at[9])
    out3.start()

    pull(4, hops[0])
    pull(MAP, hops[0] - 1)
    pull(MAP, hops[0])
    pull(5, hops[0])
    settle(4)
    tall5 = 8
    conv(m5, w_o5, ob5, r5, n * rows5, wid5, tall5)
    out5 = pltpu.make_async_copy(r5, y5, local_sem.at[10])
    out5.start()
    take = lax.broadcasted_iota(jnp.int32, (wid5 // 2, wid5), 0) * 2
    pick = (take == lax.broadcasted_iota(jnp.int32, (wid5 // 2, wid5), 1)).astype(BF16)

    def even_row(i, carry):
        row = r5[pl.ds(pl.multiple_of(2 * i * wid5, 16), wid5), :]
        r6[pl.ds(pl.multiple_of(i * (wid5 // 2), 16), wid5 // 2), :] = jnp.dot(
            pick, row, preferred_element_type=F32
        ).astype(BF16)
        return carry

    lax.fori_loop(0, n * rows5 // 2, even_row, 0)
    out6 = pltpu.make_async_copy(r6, y6, local_sem.at[11])
    out6.start()

    settle(5)
    conv(m4, w_o4, ob4, r4, rows4, wid4, rows4)
    out4 = pltpu.make_async_copy(r4, y4, local_sem.at[12])
    out4.start()

    for copy in sent:
        copy.wait_send()
    for copy in (out3, out5, out6, out4):
        copy.wait()


def on_device(n, *arrays):
    s3, s4, s5, l3, l4, l5, lb3, lb4, lb5, o3, o4, o5, ob3, ob4, ob5 = arrays
    dims = tuple(x.shape[1:3] for x in (s3, s4, s5))
    fd = l3.shape[1]
    (rows3, wid3), (rows4, wid4), (rows5, wid5) = dims
    flat = [x.reshape(-1, x.shape[3]) for x in (s3, s4, s5)]
    biases = [b.reshape(1, fd) for b in (lb3, lb4, lb5, ob3, ob4, ob5)]
    anywhere, vmem = pl.BlockSpec(memory_space=pl.ANY), pl.BlockSpec(memory_space=pltpu.VMEM)
    far = max(n // 2, 1)

    def array(*shape):
        return pltpu.VMEM(shape, BF16)

    def result(pixels):
        return jax.ShapeDtypeStruct((pixels, fd), BF16)

    dma = pltpu.SemaphoreType.DMA
    y3, y4, y5, y6 = pl.pallas_call(
        functools.partial(kernel, n, dims),
        out_shape=(
            result(rows3 * wid3),
            result(rows4 * wid4),
            result(n * rows5 * wid5),
            result(n * rows5 * wid5 // 4),
        ),
        in_specs=[anywhere] * 6 + [vmem] * 3 + [anywhere] * 3 + [vmem] * 3,
        out_specs=(anywhere,) * 4,
        scratch_shapes=[
            *(array(*x.shape) for x in flat),
            array(n * l5.shape[0], fd),
            array(n * l4.shape[0], fd),
            array(n * l3.shape[0], fd),
            *(array(3, 3, n * x.shape[2], fd) for x in (o3, o5, o4)),
            array((rows3 + 2) * wid3, fd),
            array((rows4 + 2) * wid4, fd),
            array((n * rows5 + 2) * wid5, fd),
            array(rows3 * wid3, fd),
            array(rows4 * wid4, fd),
            array(n * rows5 * wid5, fd),
            array(n * rows5 * wid5 // 4, fd),
            dma((7, 2, far)),
            dma((7, 2, far)),
            dma((6, n - 1)),
            dma((6, n - 1)),
            dma((4,)),
            dma((4,)),
            dma((13,)),
        ],
        compiler_params=pltpu.CompilerParams(
            collective_id=0, has_side_effects=True, vmem_limit_bytes=48 * 1024 * 1024
        ),
    )(*flat, l3, l4, l5, *biases[:3], o3, o4, o5, *biases[3:])
    return (
        y3.reshape(1, rows3, wid3, fd),
        y4.reshape(1, rows4, wid4, fd),
        y5.reshape(1, n * rows5, wid5, fd),
        y6.reshape(1, n * rows5 // 2, wid5 // 2, fd),
    )


def solution(mesh):
    split, rows = P("dp", "space", None, None), P("space", None)
    taps = P(None, None, "space", None)
    whole = P("dp", None, None, None)
    return jax.shard_map(
        functools.partial(on_device, mesh.shape["space"]),
        mesh=mesh,
        in_specs=(split,) * 3 + (rows,) * 3 + (P(),) * 3 + (taps,) * 3 + (P(),) * 3,
        out_specs=(split, split, whole, whole),
        check_vma=False,
    )
```

time: 204 us -> 61.8 us (0.30)
  blocking collectives: 96.2 us -> 0 us
  Pallas kernels: 0 us -> 48.7 us
  waiting for transfers between devices: 33.1 us -> 0 us
  matrix products: 15.8 us -> 0 us
  between operations: 14.3 us -> 0.71 us
  starting transfers between devices: 12.6 us -> 0 us
  local copies, waits for them, and re-layouts: 24.3 us -> 11.9 us
  other arithmetic: 6.78 us -> 0 us
    all_gather x3 -> x0, blocking collectives: 96.2 us -> none  [the longest x1 33.9 us: on_device(): lax.all_gather(lateral_four, 'space', axis=0, tiled=True)]
    pallas_call x0 -> x1, Pallas kernels: none -> 48.7 us  [on_device(): pl.pallas_call(functools.partial(kernel, n, dims), out_shape=(result(rows...]
    all_gather x4 -> x0, waiting for transfers between devices: 30.5 us -> none  [the longest x1 30.5 us: on_device(): lax.all_gather(output_three, 'space', axis=2, tiled=True)]
    dot_general x30 -> x0, matrix products: 15.8 us -> none  [the longest x27 13.5 us: conv_rows(): jnp.dot(window, weight[row_off, col_off], preferred_element_type=jnp.floa...]
    ppermute x4 -> x0, starting transfers between devices: 12.5 us -> none  [the longest x2 9.9 us: with_halo(): lax.ppermute(tail, axis, [(i, (i + 1) % count) for i in range(ends)])]
    slice x7 -> x0, local copies, waits for them, and re-layouts: 8.58 us -> none  [the longest x4 4.74 us: conv_rows(): framed[:, row_off:row_off + height, col_off:col_off + columns, :]]
    convert_element_type x5 -> x0, local copies, waits for them, and re-layouts: 5.69 us -> none  [the longest x2 3.45 us: on_device(): enlarge(merged_four).astype(jnp.float32)]
    concatenate x4 -> x0, other arithmetic: 5.37 us -> none  [with_halo(): jnp.concatenate([lax.ppermute(tail, axis, [(i, (i + 1) % count) for i in...]
  transfers between devices with their start and end apart: 8 -> 0, of which waited for: 1 -> 0; matrix products, arithmetic and copies ran while one was open for 15% -> 0% of each run, Pallas kernels for 0% -> 0%
where the time goes in v1:
time: 61.8 us; the launch traced here: 61.3 us
  Pallas kernels  48.7 us (79%)
  local copies, waits for them, and re-layouts  11.9 us (19%)
  between operations  0.71 us (1%)
    pallas_call x1, Pallas kernels, on_device(): pl.pallas_call(functools.partial(kernel, n, dims), out_shape=(result(rows...  48.7 us
    unnamed x34, local copies, waits for them, and re-layouts  11.9 us

profile of v1, /device:TPU:0, one launch (start us, length us, event | category | flops | bytes accessed | tf_op | source)
XLA Modules:
  0.0 61.3 jit_solution(2353973360878730986)
XLA Ops:
  0.6 0.0 copy-start.14
  0.6 0.0 copy-start.12
  0.7 0.0 copy-start.13
  0.7 0.0 copy-start.10
  0.7 0.0 copy-start.11
  0.7 0.0 copy-start.9
  0.7 0.6 %copy-done.14 = f32[256]{0:T(256)S(1)} copy-done((f32[256]{0:T(256)S(1)}, f32[256]{0:T(256)}, u32[]{:S(2)}) %copy-start.14) | copy-done | bytes 1048
  1.3 0.0 copy-done.12
  1.3 0.0 copy-done.13
  1.3 0.0 copy-done.10
  1.4 0.0 copy-done.11
  1.4 0.0 copy-done.9
  1.4 0.0 copy-start
  1.4 1.2 %copy-done = bf16[1,8,128,512]{3,2,1,0:T(8,128)(2,1)S(1)} copy-done((bf16[1,8,128,512]{3,2,1,0:T(8,128)(2,1)S(1)}, bf16[1,8,128,512]{3,2,1,0:T(8,128)(2,1)}, u32[]{:S(2)}) %copy-start) | copy-done | bytes 1048600
  2.6 0.0 copy-start.1
  2.6 1.0 %copy-done.1 = bf16[1,4,64,1024]{3,2,1,0:T(8,128)(2,1)S(1)} copy-done((bf16[1,4,64,1024]{3,2,1,0:T(8,128)(2,1)S(1)}, bf16[1,4,64,1024]{3,2,1,0:T(8,128)(2,1)}, u32[]{:S(2)}) %copy-start.1) | copy-done | bytes 524312
  3.7 0.0 copy-start.2
  3.7 0.9 %copy-done.2 = bf16[1,2,32,2048]{3,2,1,0:T(8,128)(2,1)S(1)} copy-done((bf16[1,2,32,2048]{3,2,1,0:T(8,128)(2,1)S(1)}, bf16[1,2,32,2048]{3,2,1,0:T(8,128)(2,1)}, u32[]{:S(2)}) %copy-start.2) | copy-done | bytes 262168
  4.6 0.0 copy-start.3
  4.6 0.9 %copy-done.3 = bf16[3,3,32,256]{3,2,1,0:T(8,128)(2,1)S(1)} copy-done((bf16[3,3,32,256]{3,2,1,0:T(8,128)(2,1)S(1)}, bf16[3,3,32,256]{3,2,1,0:T(8,128)(2,1)}, u32[]{:S(2)}) %copy-start.3) | copy-done | bytes 147480
  5.5 0.9 %copy-done.4 = bf16[3,3,32,256]{3,2,1,0:T(8,128)(2,1)S(1)} copy-done((bf16[3,3,32,256]{3,2,1,0:T(8,128)(2,1)S(1)}, bf16[3,3,32,256]{3,2,1,0:T(8,128)(2,1)}, u32[]{:S(2)}) %copy-start.4) | copy-done | bytes 147480
  6.4 0.0 copy-start.5
  6.4 0.9 %copy-done.5 = bf16[3,3,32,256]{3,2,1,0:T(8,128)(2,1)S(1)} copy-done((bf16[3,3,32,256]{3,2,1,0:T(8,128)(2,1)S(1)}, bf16[3,3,32,256]{3,2,1,0:T(8,128)(2,1)}, u32[]{:S(2)}) %copy-start.5) | copy-done | bytes 147480
  7.3 0.0 copy-start.6
  7.3 0.9 %copy-done.6 = bf16[256,256]{1,0:T(8,128)(2,1)S(1)} copy-done((bf16[256,256]{1,0:T(8,128)(2,1)S(1)}, bf16[256,256]{1,0:T(8,128)(2,1)}, u32[]{:S(2)}) %copy-start.6) | copy-done | bytes 131096
  8.3 0.8 %copy-done.7 = bf16[128,256]{1,0:T(8,128)(2,1)S(1)} copy-done((bf16[128,256]{1,0:T(8,128)(2,1)S(1)}, bf16[128,256]{1,0:T(8,128)(2,1)}, u32[]{:S(2)}) %copy-start.7) | copy-done | bytes 65560
  9.1 0.8 %copy-done.8 = bf16[64,256]{1,0:T(8,128)(2,1)S(1)} copy-done((bf16[64,256]{1,0:T(8,128)(2,1)S(1)}, bf16[64,256]{1,0:T(8,128)(2,1)}, u32[]{:S(2)}) %copy-start.8) | copy-done | bytes 32792
  9.8 48.7 %shard_map.174 = (bf16[1024,256]{1,0:T(8,128)(2,1)S(1)}, bf16[256,256]{1,0:T(8,128)(2,1)S(1)}, bf16[512,256]{1,0:T(8,128)(2,1)S(1)}, bf16[128,256]{1,0:T(8,128)(2,1)S(1)}) custom-call(bf16[1024,512]{1,0:T(8,128)(2,1)S(1)} %bitcast.13, bf16[256,1024]{1,0:T(8,128)(2,1)S(1)} %bitcast.15, bf16[64,2048]{1,0:T(8,128)(2,1)S(1)} %bitcast.17, ...), custom_call_target="tpu_custom_call" | custom-call | tf_op jit(solution)/shard_map/pallas_call | solution.py:306
  58.5 0.8 %copy.23 = bf16[1,8,128,256]{3,2,1,0:T(8,128)(2,1)} copy(bf16[1,8,128,256]{3,2,1,0:T(8,128)(2,1)S(1)} %bitcast.14) | data formatting | bytes 1048576
  59.3 0.7 %copy.24 = bf16[1,4,64,256]{3,2,1,0:T(8,128)(2,1)} copy(bf16[1,4,64,256]{3,2,1,0:T(8,128)(2,1)S(1)} %bitcast.18) | data formatting | bytes 262144
  60.0 0.7 %copy.25 = bf16[1,16,32,256]{3,2,1,0:T(8,128)(2,1)} copy(bf16[1,16,32,256]{3,2,1,0:T(8,128)(2,1)S(1)} %bitcast.16) | data formatting | bytes 524288
  60.7 0.6 %copy.26 = bf16[1,8,16,256]{3,2,1,0:T(8,128)(2,1)} copy(bf16[1,8,16,256]{3,2,1,0:T(8,128)(2,1)S(1)} %bitcast.19) | data formatting | bytes 131072
  (3 shorter events, 0.0 us)
Async XLA Ops:
  0.6 0.7 %copy-start.14 = (f32[256]{0:T(256)S(1)}, f32[256]{0:T(256)}, u32[]{:S(2)}) copy-start(f32[256]{0:T(256)} %param.29) | copy-start | bytes 3076
  0.6 0.7 %copy-start.12 = (f32[256]{0:T(256)S(1)}, f32[256]{0:T(256)}, u32[]{:S(2)}) copy-start(f32[256]{0:T(256)} %param.27) | copy-start | bytes 3076
  0.7 0.7 %copy-start.13 = (f32[256]{0:T(256)S(1)}, f32[256]{0:T(256)}, u32[]{:S(2)}) copy-start(f32[256]{0:T(256)} %param.28) | copy-start | bytes 3076
  0.7 0.7 %copy-start.10 = (f32[256]{0:T(256)S(1)}, f32[256]{0:T(256)}, u32[]{:S(2)}) copy-start(f32[256]{0:T(256)} %param.22) | copy-start | bytes 3076
  0.7 0.7 %copy-start.11 = (f32[256]{0:T(256)S(1)}, f32[256]{0:T(256)}, u32[]{:S(2)}) copy-start(f32[256]{0:T(256)} %param.23) | copy-start | bytes 3076
  0.7 0.7 %copy-start.9 = (f32[256]{0:T(256)S(1)}, f32[256]{0:T(256)}, u32[]{:S(2)}) copy-start(f32[256]{0:T(256)} %param.21) | copy-start | bytes 3076
  1.4 1.2 %copy-start = (bf16[1,8,128,512]{3,2,1,0:T(8,128)(2,1)S(1)}, bf16[1,8,128,512]{3,2,1,0:T(8,128)(2,1)}, u32[]{:S(2)}) copy-start(bf16[1,8,128,512]{3,2,1,0:T(8,128)(2,1)} %param.15) | copy-start | bytes 3145732
  2.6 1.0 %copy-start.1 = (bf16[1,4,64,1024]{3,2,1,0:T(8,128)(2,1)S(1)}, bf16[1,4,64,1024]{3,2,1,0:T(8,128)(2,1)}, u32[]{:S(2)}) copy-start(bf16[1,4,64,1024]{3,2,1,0:T(8,128)(2,1)} %param.16) | copy-start | bytes 1572868
  3.7 0.9 %copy-start.2 = (bf16[1,2,32,2048]{3,2,1,0:T(8,128)(2,1)S(1)}, bf16[1,2,32,2048]{3,2,1,0:T(8,128)(2,1)}, u32[]{:S(2)}) copy-start(bf16[1,2,32,2048]{3,2,1,0:T(8,128)(2,1)} %param.17) | copy-start | bytes 786436
  4.6 0.9 %copy-start.3 = (bf16[3,3,32,256]{3,2,1,0:T(8,128)(2,1)S(1)}, bf16[3,3,32,256]{3,2,1,0:T(8,128)(2,1)}, u32[]{:S(2)}) copy-start(bf16[3,3,32,256]{3,2,1,0:T(8,128)(2,1)} %o3.1) | copy-start | bytes 442372
  5.5 0.9 %copy-start.4 = (bf16[3,3,32,256]{3,2,1,0:T(8,128)(2,1)S(1)}, bf16[3,3,32,256]{3,2,1,0:T(8,128)(2,1)}, u32[]{:S(2)}) copy-start(bf16[3,3,32,256]{3,2,1,0:T(8,128)(2,1)} %o4.1) | copy-start | bytes 442372
  6.4 0.9 %copy-start.5 = (bf16[3,3,32,256]{3,2,1,0:T(8,128)(2,1)S(1)}, bf16[3,3,32,256]{3,2,1,0:T(8,128)(2,1)}, u32[]{:S(2)}) copy-start(bf16[3,3,32,256]{3,2,1,0:T(8,128)(2,1)} %o5.1) | copy-start | bytes 442372
  7.3 0.9 %copy-start.6 = (bf16[256,256]{1,0:T(8,128)(2,1)S(1)}, bf16[256,256]{1,0:T(8,128)(2,1)}, u32[]{:S(2)}) copy-start(bf16[256,256]{1,0:T(8,128)(2,1)} %l5.1) | copy-start | bytes 393220
  8.3 0.8 %copy-start.7 = (bf16[128,256]{1,0:T(8,128)(2,1)S(1)}, bf16[128,256]{1,0:T(8,128)(2,1)}, u32[]{:S(2)}) copy-start(bf16[128,256]{1,0:T(8,128)(2,1)} %l4.1) | copy-start | bytes 196612
  9.1 0.8 %copy-start.8 = (bf16[64,256]{1,0:T(8,128)(2,1)S(1)}, bf16[64,256]{1,0:T(8,128)(2,1)}, u32[]{:S(2)}) copy-start(bf16[64,256]{1,0:T(8,128)(2,1)} %l3.1) | copy-start | bytes 98308

commit v2 on v1

--- a/solution.py
+++ b/solution.py
@@ -48,11 +48,11 @@
 
 def kernel(
     n, dims,
-    s3, s4, s5, l3, l4, l5, lb3, lb4, lb5, o3, o4, o5, ob3, ob4, ob5,
+    s3, s4, s5, l3, l4, l5, hb3, hb4, hb5, o3, o4, o5, hc3, hc4, hc5,
     y3, y4, y5, y6,
     v3, v4, v5, w_l5, w_l4, w_l3, w_o3, w_o5, w_o4,
-    m3, m4, m5, r3, r4, r5, r6,
-    ring_send, ring_recv, core_send, core_recv, halo_send, halo_recv, local_sem,
+    m3, m4, m5, r3, r4, r5, r6, lb3, lb4, lb5, ob3, ob4, ob5,
+    ring_send, ring_recv, core_send, core_recv, map_send, map_recv, halo_send, halo_recv, local_sem,
 ):
     (rows3, wid3), (rows4, wid4), (rows5, wid5) = dims
     dp, s = lax.axis_index("dp"), lax.axis_index("space")
@@ -65,16 +65,16 @@
     target = [(dp, ring_owner(place + turn[k], n)) for k in range(2)]
     above, below = (dp, (s + n - 1) % n), (dp, (s + 1) % n)
 
-    full = (w_l5, w_l4, w_l3, w_o3, w_o5, w_o4, m5)
+    full = (w_l5, w_l4, w_l3, w_o3, w_o5, w_o4)
     mine = (l5, l4, l3, o3, o5, o4)
     half = w_l5.shape[1] // 2
-    MAP = 6
+
+    def map_rows(owner):
+        size = rows5 * wid5
+        return m5.at[pl.ds(pl.multiple_of(wid5 + owner * size, 16), size), :]
 
     def chunk(a, owner, side):
         cols = pl.ds(pl.multiple_of(side * half, half), half)
-        if a == MAP:
-            size = rows5 * wid5
-            return m5.at[pl.ds(pl.multiple_of(wid5 + owner * size, 16), size), :]
         if a < 3:
             size = mine[a].shape[0]
             return full[a].at[pl.ds(pl.multiple_of(owner * size, size), size), cols]
@@ -97,15 +97,22 @@
         pltpu.make_async_copy(src, dst, local_sem.at[6 + k])
         for k, (src, dst) in enumerate(((s5, v5), (s4, v4), (s3, v3)))
     ]
-    for copy in features + local:
+    biases = [
+        pltpu.make_async_copy(src, dst, local_sem.at[13 + k])
+        for k, (src, dst) in enumerate(
+            ((hb3, lb3), (hb4, lb4), (hb5, lb5), (hc3, ob3), (hc4, ob4), (hc5, ob5))
+        )
+    ]
+    for copy in features + local + biases:
         copy.start()
 
     barrier = pltpu.get_barrier_semaphore()
-    for device in (target[0], target[1], partner, above, below):
+    peers = [(dp, (s + d) % n) for d in range(1, n)]
+    for device in (*peers, partner):
         pl.semaphore_signal(
             barrier, inc=1, device_id=device, device_id_type=pl.DeviceIdType.MESH
         )
-    pl.semaphore_wait(barrier, 5)
+    pl.semaphore_wait(barrier, n)
 
     def remote(src, dst, send, recv, device):
         return pltpu.make_async_remote_copy(
@@ -120,7 +127,7 @@
             return
         owner = ring_owner(place - turn[k] * (step - 1), n)
         dst = chunk(a, owner, core)
-        src = own_part(a) if step == 1 and a != MAP else dst
+        src = own_part(a) if step == 1 else dst
         copy = remote(src, dst, ring_send.at[a, k, step - 1], ring_recv.at[a, k, step - 1], target[k])
         copy.start()
         sent.append(copy)
@@ -141,10 +148,9 @@
                 spot, spot, ring_send.at[a, k, step - 1], ring_recv.at[a, k, step - 1], target[k]
             ).wait_recv()
             push(a, k, step + 1)
-            if a != MAP:
-                copy = cross(a, k, step, core, turn)
-                copy.start()
-                sent.append(copy)
+            copy = cross(a, k, step, core, turn)
+            copy.start()
+            sent.append(copy)
 
     def settle(a):
         for k in range(2):
@@ -157,7 +163,7 @@
         push(a, 1, 1)
     waiting = [3, 4, 5]
     for step in range(1, hops[0] + 1):
-        if waiting:
+        if waiting and step > 1:
             a = waiting.pop(0)
             push(a, 0, 1)
             push(a, 1, 1)
@@ -172,6 +178,8 @@
 
     settle(0)
     features[0].wait()
+    for copy in biases:
+        copy.wait()
     zero5 = jnp.zeros((wid5, m5.shape[1]), BF16)
     m5[pl.ds(0, wid5), :] = zero5
     m5[pl.ds(m5.shape[0] - wid5, wid5), :] = zero5
@@ -181,6 +189,10 @@
     ).astype(BF16)
     settle(1)
     features[1].wait()
+    for d in range(1, n):
+        copy = remote(map_rows(s), map_rows(s), map_send.at[d - 1], map_recv.at[d - 1], peers[d - 1])
+        copy.start()
+        sent.append(copy)
     for r in range(rows5):
         up = spread(m5[pl.ds(pl.multiple_of(here + r * wid5, 16), wid5), :])
         base = 2 * r * wid4
@@ -188,8 +200,6 @@
         m4[wid4 + base : wid4 + base + 2 * wid4, :] = (
             lat + lb4[...] + jnp.concatenate([up, up], axis=0)
         ).astype(BF16)
-    push(MAP, 0, 1)
-    push(MAP, 1, 1)
     settle(2)
     features[2].wait()
 
@@ -202,7 +212,10 @@
         ).astype(BF16)
         return carry
 
-    lax.fori_loop(0, rows4, coarse_row, 0)
+    lax.fori_loop(0, rows4 // 2, coarse_row, 0)
+    for a in (3, 4, 5):
+        pull(a, 2)
+    lax.fori_loop(rows4 // 2, rows4, coarse_row, 0)
 
     halos = []
     for k, (frame, rows, wid) in enumerate(((m4, rows4, wid4), (m3, rows3, wid3))):
@@ -212,20 +225,38 @@
             remote(last, top, halo_send.at[2 * k], halo_recv.at[2 * k], below),
             remote(first, bottom, halo_send.at[2 * k + 1], halo_recv.at[2 * k + 1], above),
         ))
-    for step in range(2, hops[0]):
+
+    def start_halos():
+        @pl.when(s < n - 1)
+        def _():
+            for pair in halos:
+                pair[0].start()
+
+        @pl.when(s > 0)
+        def _():
+            for pair in halos:
+                pair[1].start()
+
+    for step in range(3, hops[0]):
         for a in (3, 4, 5):
             pull(a, step)
-        if step == 2:
-            for pair in halos:
-                for copy in pair:
-                    copy.start()
-        pull(MAP, step - 1)
+            if step == 3 and a == 3:
+                start_halos()
     pull(3, hops[0])
 
-    for pair, frame, rows, wid in zip(halos, (m4, m3), (rows4, rows3), (wid4, wid3)):
-        for copy in pair:
-            copy.wait_recv()
-            sent.append(copy)
+    @pl.when(s > 0)
+    def _():
+        for pair in halos:
+            pair[0].wait_recv()
+            pair[1].wait_send()
+
+    @pl.when(s < n - 1)
+    def _():
+        for pair in halos:
+            pair[1].wait_recv()
+            pair[0].wait_send()
+
+    for frame, rows, wid in ((m4, rows4, wid4), (m3, rows3, wid3)):
         zero = jnp.zeros((wid, frame.shape[1]), BF16)
 
         @pl.when(s == 0)
@@ -248,17 +279,17 @@
 
         lax.fori_loop(0, rows // tall, tile, 0)
 
-    conv(m3, w_o3, ob3, r3, rows3, wid3, 2)
+    conv(m3, w_o3, ob3, r3, rows3, wid3, 4)
     out3 = pltpu.make_async_copy(r3, y3, local_sem.at[9])
     out3.start()
 
     pull(4, hops[0])
-    pull(MAP, hops[0] - 1)
-    pull(MAP, hops[0])
     pull(5, hops[0])
     settle(4)
-    tall5 = 8
-    conv(m5, w_o5, ob5, r5, n * rows5, wid5, tall5)
+    for d in range(1, n):
+        spot = map_rows((s + n - d) % n)
+        remote(spot, spot, map_send.at[d - 1], map_recv.at[d - 1], peers[d - 1]).wait_recv()
+    conv(m5, w_o5, ob5, r5, n * rows5, wid5, 16)
     out5 = pltpu.make_async_copy(r5, y5, local_sem.at[10])
     out5.start()
     take = lax.broadcasted_iota(jnp.int32, (wid5 // 2, wid5), 0) * 2
@@ -293,7 +324,7 @@
     (rows3, wid3), (rows4, wid4), (rows5, wid5) = dims
     flat = [x.reshape(-1, x.shape[3]) for x in (s3, s4, s5)]
     biases = [b.reshape(1, fd) for b in (lb3, lb4, lb5, ob3, ob4, ob5)]
-    anywhere, vmem = pl.BlockSpec(memory_space=pl.ANY), pl.BlockSpec(memory_space=pltpu.VMEM)
+    anywhere = pl.BlockSpec(memory_space=pl.ANY)
     far = max(n // 2, 1)
 
     def array(*shape):
@@ -311,7 +342,7 @@
             result(n * rows5 * wid5),
             result(n * rows5 * wid5 // 4),
         ),
-        in_specs=[anywhere] * 6 + [vmem] * 3 + [anywhere] * 3 + [vmem] * 3,
+        in_specs=[anywhere] * 15,
         out_specs=(anywhere,) * 4,
         scratch_shapes=[
             *(array(*x.shape) for x in flat),
@@ -326,16 +357,19 @@
             array(rows4 * wid4, fd),
             array(n * rows5 * wid5, fd),
             array(n * rows5 * wid5 // 4, fd),
-            dma((7, 2, far)),
-            dma((7, 2, far)),
+            *(pltpu.VMEM((1, fd), F32) for _ in range(6)),
+            dma((6, 2, far)),
+            dma((6, 2, far)),
             dma((6, n - 1)),
             dma((6, n - 1)),
+            dma((n - 1,)),
+            dma((n - 1,)),
             dma((4,)),
             dma((4,)),
-            dma((13,)),
+            dma((19,)),
         ],
         compiler_params=pltpu.CompilerParams(
-            collective_id=0, has_side_effects=True, vmem_limit_bytes=48 * 1024 * 1024
+            collective_id=0, has_side_effects=True, vmem_limit_bytes=60 * 1024 * 1024
         ),
     )(*flat, l3, l4, l5, *biases[:3], o3, o4, o5, *biases[3:])
     return (

time: 61.8 us -> 52.3 us (0.85)
  the two profiles are of different devices: /device:TPU:0 before, /device:TPU:15 now
where the time goes in v2:
time: 52.3 us; the launch traced here: 52.1 us
  Pallas kernels  47.1 us (90%)
  local copies, waits for them, and re-layouts  4.4 us (8%)
  between operations  0.66 us (1%)
    pallas_call x1, Pallas kernels, on_device(): pl.pallas_call(functools.partial(kernel, n, dims), out_shape=(result(rows...  47.1 us
    unnamed x10, local copies, waits for them, and re-layouts  4.4 us

profile of v2, /device:TPU:15, one launch (start us, length us, event | category | flops | bytes accessed | tf_op | source)
XLA Modules:
  0.0 52.1 jit_solution(2948003459830567740)
XLA Ops:
  0.6 47.1 %shard_map.174 = (bf16[1024,256]{1,0:T(8,128)(2,1)}, bf16[256,256]{1,0:T(8,128)(2,1)}, bf16[512,256]{1,0:T(8,128)(2,1)}, bf16[128,256]{1,0:T(8,128)(2,1)}) custom-call(bf16[1024,512]{1,0:T(8,128)(2,1)} %bitcast.13, bf16[256,1024]{1,0:T(8,128)(2,1)} %bitcast.15, bf16[64,2048]{1,0:T(8,128)(2,1)} %bitcast.17, bf16[64,256]{1,0:T(8,128)(2,1)} %l3.1, ...), custom_call_target="tpu_custom_call" | custom-call | tf_op jit(solution)/shard_map/pallas_call | solution.py:337
  47.7 0.0 copy-start.1
  47.7 1.9 %copy.23 = bf16[1,8,128,256]{3,2,1,0:T(8,128)(2,1)} copy(bf16[1,8,128,256]{3,2,1,0:T(8,128)(2,1)} %bitcast.14) | data formatting | bytes 1048576
  49.6 0.0 copy-done.1
  49.6 0.0 copy-start
  49.6 0.7 %copy.24 = bf16[1,4,64,256]{3,2,1,0:T(8,128)(2,1)} copy(bf16[1,4,64,256]{3,2,1,0:T(8,128)(2,1)S(1)} %bitcast.18) | data formatting | bytes 262144
  50.3 0.3 copy-done
  50.6 0.0 copy-start.2
  50.6 0.7 %copy.25 = bf16[1,16,32,256]{3,2,1,0:T(8,128)(2,1)} copy(bf16[1,16,32,256]{3,2,1,0:T(8,128)(2,1)S(1)} %bitcast.16) | data formatting | bytes 524288
  51.3 0.2 copy-done.2
  51.5 0.6 %copy.26 = bf16[1,8,16,256]{3,2,1,0:T(8,128)(2,1)} copy(bf16[1,8,16,256]{3,2,1,0:T(8,128)(2,1)S(1)} %bitcast.19) | data formatting | bytes 131072
Async XLA Ops:
  47.7 1.9 %copy-start.1 = (bf16[256,256]{1,0:T(8,128)(2,1)S(1)}, bf16[256,256]{1,0:T(8,128)(2,1)}, u32[]{:S(2)}) copy-start(bf16[256,256]{1,0:T(8,128)(2,1)} %get-tuple-element.9) | copy-start | bytes 393220
  49.6 1.0 %copy-start = (bf16[512,256]{1,0:T(8,128)(2,1)S(1)}, bf16[512,256]{1,0:T(8,128)(2,1)}, u32[]{:S(2)}) copy-start(bf16[512,256]{1,0:T(8,128)(2,1)} %get-tuple-element.10) | copy-start | bytes 786436
  50.6 0.9 %copy-start.2 = (bf16[128,256]{1,0:T(8,128)(2,1)S(1)}, bf16[128,256]{1,0:T(8,128)(2,1)}, u32[]{:S(2)}) copy-start(bf16[128,256]{1,0:T(8,128)(2,1)} %get-tuple-element.11) | copy-start | bytes 196612
